TPU v7x, 128 devices: a whole 4x4x4 slice. The times are simulated.
128 devices in a mesh: neg: 16 (over x, y), qry: 8 (over z, core).
Axes of the slice: x: 4, y: 4, z: 4, core: 2. Of those that a mesh axis runs over, the one named last changes fastest.
Arguments:
- items_table: bfloat16 [131072, 512], P('neg'), may hold values from -6 to 6
- fetch_rows: int32 [2048, 640], P(('neg', 'qry')), may hold values from 0 to 8191, as said below
- neighbour_slots: int32 [65536, 40], P(('neg', 'qry')), may hold values from 0 to 10239, as said below
- neighbour_count: int32 [65536], P(('neg', 'qry')), may hold values from 20 to 40
- self_slot: int32 [65536], P(('neg', 'qry')), may hold values from 0 to 10239
- negative_count: int32 [65536], P('neg'), may hold values from 1 to 999
- message_weight: bfloat16 [512, 512], replicated, may hold values from -0.25 to 0.25
- message_bias: float32 [512], replicated, may hold values from -3 to 3
- self_weight: bfloat16 [512, 512], replicated, may hold values from -0.25 to 0.25
- neighbour_weight: bfloat16 [512, 512], replicated, may hold values from -0.25 to 0.25
- output_bias: float32 [512], replicated, may hold values from -3 to 3
- queries: bfloat16 [8192, 512], P('qry'), may hold values from -8 to 8
Outputs:
- negative_embed: bfloat16 [65536, 512], P(('neg', 'qry'))
- query_lse: float32 [8192], P('qry')
Inputs may be any that keep to these rules, and one draw needn't show every extreme that they name: Within one row of fetch_rows (one device's list for one partition) no item appears twice. `neighbour_slots`: every one of a device's 16 * 640 fetched rows is named by at least one live neighbour of that device's negatives.
All inputs are finite; a program needn't handle non-finite values.
Results may differ from a plain program's by a relative error of at most 0.0055.
Values may be sent and summed in bfloat16 or wider, within the bound.
No kernel may reach another device: no remote copies, remote signals or barrier semaphores. Data moves between devices by JAX's collectives and lax.ppermute only.
A program may use at most 128 MiB of HBM per device.

v0:
```python
import math

import jax
import jax.numpy as jnp
from jax import lax
from jax.sharding import PartitionSpec as P


def from_everyone(x, axis):
    devices = lax.axis_size(axis)
    return lax.all_to_all(jnp.broadcast_to(x[None], (devices, *x.shape)), axis, 0, 0, tiled=True)


def gathered_once(x, axis):
    leaves = jax.tree.leaves(x)
    sequence = sorted(range(len(leaves)), key=lambda k: -leaves[k].size)
    width = (1, *leaves[sequence[0]].shape)[-1]
    lines = [
        jnp.pad(leaves[k].reshape(-1), (0, -leaves[k].size % width)).reshape(-1, width)
        for k in sequence
    ]
    both, at, found = (from_everyone(jnp.concatenate(lines), axis), 0, {})
    for k, line in zip(sequence, lines):
        slab = both[:, at : at + len(line)].reshape(len(both), -1)
        found[k] = slab[:, : leaves[k].size].reshape(-1, *leaves[k].shape)
        at += len(line)
    numbers = iter(range(len(leaves)))
    return jax.tree.map(lambda _: found[next(numbers)], x)


def joined_by_halves(pieces, combine):
    while len(jax.tree.leaves(pieces)[0]) > 1:
        pieces = jax.vmap(combine)(
            *(jax.tree.map(lambda part: part[side::2], pieces) for side in (0, 1))
        )
    return jax.tree.map(lambda part: part[0], pieces)


def merged(x, axis, combine):
    pieces = gathered_once(x, axis)
    return joined_by_halves(pieces, combine)


def pair_join(first, second):
    top_value = jnp.maximum(first[0], second[0])
    return (
        top_value,
        first[1] * jnp.exp(first[0] - top_value) + second[1] * jnp.exp(second[0] - top_value),
    )


def combine_column(peak, totals):
    return merged((peak, totals), "neg", pair_join)


def score_against(query_part, negative_part):
    return lax.dot_general(
        query_part, negative_part, (((1,), (1,)), ((), ())), preferred_element_type=jnp.float32
    )


def make_message(rows, message_weight, message_bias):
    return jax.nn.relu(
        jnp.dot(rows, message_weight, preferred_element_type=jnp.float32) + message_bias
    ).astype(jnp.bfloat16)


def per_device(
    items_table,
    fetch_rows,
    neighbour_slots,
    neighbour_count,
    self_slot,
    negative_count,
    message_weight,
    message_bias,
    self_weight,
    neighbour_weight,
    output_bias,
    queries,
):
    width = items_table.shape[1]
    neighbours = neighbour_slots.shape[1]
    live_mask = jnp.arange(neighbours, dtype=jnp.int32)[None, :] < neighbour_count[:, None]
    served = items_table[lax.all_to_all(fetch_rows, "neg", split_axis=0, concat_axis=0, tiled=True)]
    fetched = lax.all_to_all(served, "neg", split_axis=0, concat_axis=0, tiled=True)
    fetched = fetched.reshape(-1, width)
    message = make_message(fetched, message_weight, message_bias)
    gathered = message[neighbour_slots]
    summed = jnp.sum(
        jnp.where(live_mask[:, :, None], gathered, jnp.zeros((), jnp.bfloat16)),
        axis=1,
        dtype=jnp.float32,
    )
    self_rows = fetched[self_slot]
    neighbour_mean = (summed / neighbour_count.astype(jnp.float32)[:, None]).astype(jnp.bfloat16)
    hidden = jnp.dot(self_rows, self_weight, preferred_element_type=jnp.float32)
    hidden = (
        hidden
        + jnp.dot(neighbour_mean, neighbour_weight, preferred_element_type=jnp.float32)
        + output_bias
    )
    hidden = jax.nn.relu(hidden)
    scale_inv = lax.rsqrt(jnp.mean(hidden * hidden, axis=-1, keepdims=True) + 0.25)
    negative_embed = (hidden * scale_inv).astype(jnp.bfloat16)
    log_count = jnp.log(negative_count.astype(jnp.float32))
    negatives_all = log_count.shape[0] * lax.axis_size("neg")
    query_rows_own = queries.shape[0]
    peak_old = jnp.full((query_rows_own,), -1e30, jnp.float32)
    scores = (
        0.25 * score_against(queries, lax.all_gather(negative_embed, "qry", axis=0, tiled=True))
        - log_count[None, :]
    )
    peak_new = jnp.maximum(peak_old, jnp.max(scores, axis=1))
    totals_new = jnp.sum(jnp.exp(scores - peak_new[:, None]), axis=1)
    peak = peak_new
    totals = totals_new
    peak, totals = combine_column(peak, totals)
    query_lse = peak + jnp.log(totals) - math.log(negatives_all)
    return (negative_embed, query_lse)


def solution(mesh):
    in_specs = (
        P("neg", None),
        P(("neg", "qry"), None),
        P(("neg", "qry"), None),
        P(("neg", "qry")),
        P(("neg", "qry")),
        P("neg"),
        P(),
        P(),
        P(),
        P(),
        P(),
        P("qry", None),
    )
    out_specs = (P(("neg", "qry"), None), P("qry"))
    return jax.shard_map(
        per_device, mesh=mesh, in_specs=in_specs, out_specs=out_specs, check_vma=False
    )
```

profile of v0, /device:TPU:1, one launch (start us, length us, event | category | flops | bytes accessed | tf_op | source)
XLA Modules:
  0.0 450.2 jit_solution(16907306595817737772)
XLA Ops:
  7.2 0.0 copy-start
  7.2 0.9 all_to_all.14
  8.1 13.9 %all_to_all.22 = s32[16,1,640]{2,1,0:T(1,128)S(1)} all-to-all(s32[16,1,640]{2,1,0:T(1,128)S(1)} %all_to_all.14), channel_id=1, replica_groups=mesh['neg'=16,'qry'=8] {'neg'}, dimensions={0} | all-to-all | bytes 81920 | tf_op jit(solution)/shard_map/all_to_all | solution.py:85
  22.0 46.5 %gather_fusion = bf16[10240,512]{1,0:T(8,128)(2,1)} fusion(bf16[8192,512]{1,0:T(8,128)(2,1)} %param.12, s32[10240]{0:T(1024)S(1)} %broadcast_clamp_fusion.1), kind=kCustom, calls=%fused_computation | custom fusion | bytes 21012480 | tf_op jit(solution)/shard_map/gather | solution.py:85
  68.5 0.0 copy-start.3
  68.5 0.0 copy-start.5
  68.5 0.0 copy-start.6
  68.5 0.0 copy-start.2
  68.6 0.0 copy-start.8
  68.6 5.0 %all-to-all-start.1 = ((bf16[16,640,512]{2,1,0:T(8,128)(2,1)}), bf16[16,640,512]{2,1,0:T(8,128)(2,1)}, u32[]{:S(2)}, u32[]{:S(2)}) async-start(bf16[16,640,512]{2,1,0:T(8,128)(2,1)} %bitcast.21), calls=%async_computation.1 | async-start | bytes 20971520 | tf_op jit(solution)/shard_map/all_to_all | solution.py:86
  73.6 0.0 all-gather.2.cloned.1.call-start
  73.6 0.0 copy-done.3
  73.6 0.1 copy.19
  73.8 0.2 reshape.119
  74.0 0.0 copy-done.5
  74.0 0.0 copy-done.6
  74.0 0.1 iota_compare_fusion
  74.2 173.9 %all-to-all-done.1 = bf16[16,640,512]{2,1,0:T(8,128)(2,1)} async-done(((bf16[16,640,512]{2,1,0:T(8,128)(2,1)}), bf16[16,640,512]{2,1,0:T(8,128)(2,1)}, u32[]{:S(2)}, u32[]{:S(2)}) %all-to-all-start.1) | async-done | bytes 10485792 | tf_op jit(solution)/shard_map/all_to_all | solution.py:86
  248.1 7.5 %gather_fusion.1 = bf16[512,512]{1,0:T(8,128)(2,1)S(1)} fusion(bf16[10240,512]{1,0:T(8,128)(2,1)} %bitcast.3, s32[1024]{0:T(1024)S(1)} %pad_clamp_fusion), kind=kCustom, calls=%fused_computation.1 | custom fusion | bytes 1050624 | tf_op jit(solution)/shard_map/gather | solution.py:95
  255.6 0.0 copy-done.2
  255.6 0.5 fusion.7
  256.1 0.0 copy-done.8
  256.1 10.8 %maximum_convert_fusion = bf16[10240,512]{1,0:T(8,128)(2,1)} fusion(bf16[10240,512]{1,0:T(8,128)(2,1)} %bitcast.3, bf16[512,512]{1,0:T(8,128)(2,1)} %param.18, f32[512]{0:T(512)S(1)} %copy-done.8), kind=kOutput, calls=%fused_computation.4 | convolution fusion | flops 5384437760 | bytes 21497856 | tf_op jit(solution)/shard_map/dot_general | solution.py:64
  266.9 88.5 %gather_fusion.2 = bf16[20480,512]{1,0:T(8,128)(2,1)} fusion(bf16[10240,512]{1,0:T(8,128)(2,1)} %maximum_convert_fusion, s32[20480]{0:T(1024)S(1)} %broadcast_clamp_fusion), kind=kCustom, calls=%fused_computation.2 | custom fusion | bytes 42024960 | tf_op jit(solution)/shard_map/gather | solution.py:89
  355.4 0.0 copy-start.7
  355.4 0.0 copy-start.9
  355.4 0.0 copy-start.4
  355.4 17.6 %convert_reduce_fusion = f32[512,512]{1,0:T(8,128)S(1)} fusion(bf16[512,40,512]{2,1,0:T(8,128)(2,1)} %bitcast.20, pred[512,40]{1,0:T(8,128)(4,1)S(1)} %iota_compare_fusion), kind=kLoop, calls=%fused_computation.3 | loop fusion | flops 31195136 | bytes 22040576 | tf_op jit(solution)/shard_map/reduce_sum | solution.py:90
  373.1 0.0 copy-done.7
  373.1 0.0 copy-done.9
  373.1 0.6 multiply_reduce_fusion
  373.7 0.9 multiply_convert_fusion
  374.6 0.0 all-gather.2.cloned.1.call-update
  374.7 0.0 copy-done.4
  374.7 41.5 %all-gather.2.cloned.1.call-done = bf16[4096,512]{0,1:T(8,128)(2,1)} async-done(((bf16[512,512]{0,1:T(8,128)(2,1)}), bf16[4096,512]{0,1:T(8,128)(2,1)}) %all-gather.2.cloned.1.call-update) | async-done | bytes 4194320 | tf_op jit(solution)/shard_map/all_gather | solution.py:111
  416.2 0.0 copy-done
  416.2 8.4 %fusion = (f32[1024]{0:T(1024)S(1)}, f32[4096,1024]{1,0:T(8,128)S(1)}) fusion(f32[4096]{0:T(1024)S(1)} %convert_log_fusion, bf16[4096,512]{0,1:T(8,128)(2,1)} %all-gather.2.cloned.1.call-done, bf16[1024,512]{1,0:T(8,128)(2,1)S(1)} %copy-done), kind=kOutput, calls=%fused_computation.7 | convolution fusion | flops 4307549184 | bytes 22040576 | tf_op jit(solution)/shard_map/dot_general | solution.py:57
  424.6 0.0 copy-start.1
  424.6 3.6 exponential_reduce_fusion
  428.2 0.7 broadcast_in_dim.42
  428.9 6.5 %all-to-all-start.2 = ((f32[16,2,1024]{2,1,0:T(2,128)}), f32[16,2,1024]{2,1,0:T(2,128)S(1)}, u32[]{:S(2)}, u32[]{:S(2)}) async-start(f32[16,2,1024]{2,1,0:T(2,128)} %broadcast_in_dim.42), calls=%async_computation.2 | async-start | bytes 262144 | tf_op jit(solution)/shard_map/all_to_all | solution.py:11
  435.5 0.0 copy-done.1
  435.5 1.0 copy.21
  436.5 5.7 %all-to-all-done.2 = f32[16,2,1024]{2,1,0:T(2,128)S(1)} async-done(((f32[16,2,1024]{2,1,0:T(2,128)}), f32[16,2,1024]{2,1,0:T(2,128)S(1)}, u32[]{:S(2)}, u32[]{:S(2)}) %all-to-all-start.2) | async-done | bytes 131104 | tf_op jit(solution)/shard_map/all_to_all | solution.py:11
  442.2 0.1 fusion.6
  442.7 0.6 add_add_fusion
  (27 shorter events, 0.5 us)
Async XLA Ops:
  7.2 409.0 %copy-start = (bf16[1024,512]{1,0:T(8,128)(2,1)S(1)}, bf16[1024,512]{1,0:T(8,128)(2,1)}, u32[]{:S(2)}) copy-start(bf16[1024,512]{1,0:T(8,128)(2,1)} %param.23) | copy-start | bytes 3145732
  68.5 5.1 %copy-start.3 = (s32[512,40]{0,1:T(8,128)S(1)}, s32[512,40]{0,1:T(8,128)}, u32[]{:S(2)}) copy-start(s32[512,40]{0,1:T(8,128)} %param.14) | copy-start | bytes 245764
  68.5 5.4 %copy-start.5 = (s32[512]{0:T(512)S(1)}, s32[512]{0:T(512)}, u32[]{:S(2)}) copy-start(s32[512]{0:T(512)} %param.15) | copy-start | bytes 6148
  68.5 5.4 %copy-start.6 = (s32[512]{0:T(512)S(1)}, s32[512]{0:T(512)}, u32[]{:S(2)}) copy-start(s32[512]{0:T(512)} %param.16) | copy-start | bytes 6148
  68.5 187.1 %copy-start.2 = (bf16[512,512]{1,0:T(8,128)(2,1)S(1)}, bf16[512,512]{1,0:T(8,128)(2,1)}, u32[]{:S(2)}) copy-start(bf16[512,512]{1,0:T(8,128)(2,1)} %param.20) | copy-start | bytes 1572868
  68.6 187.5 %copy-start.8 = (f32[512]{0:T(512)S(1)}, f32[512]{0:T(512)}, u32[]{:S(2)}) copy-start(f32[512]{0:T(512)} %param.19) | copy-start | bytes 6148
  68.6 179.5 %all-to-all-start.1 = ((bf16[16,640,512]{2,1,0:T(8,128)(2,1)}), bf16[16,640,512]{2,1,0:T(8,128)(2,1)}, u32[]{:S(2)}, u32[]{:S(2)}) async-start(bf16[16,640,512]{2,1,0:T(8,128)(2,1)} %bitcast.21), calls=%async_computation.1 | async-start | bytes 20971520 | tf_op jit(solution)/shard_map/all_to_all | solution.py:86
  73.6 342.6 %all-gather.2.cloned.1.call-start = ((), (), s32[]{:S(2)}) async-start(), calls=%async_computation.3 | async-start | bytes 4718592 | tf_op jit(solution)/shard_map/all_gather | solution.py:111
  355.4 17.7 %copy-start.7 = (bf16[512,512]{1,0:T(8,128)(2,1)S(1)}, bf16[512,512]{1,0:T(8,128)(2,1)}, u32[]{:S(2)}) copy-start(bf16[512,512]{1,0:T(8,128)(2,1)} %param.21) | copy-start | bytes 1572868
  355.4 17.7 %copy-start.9 = (f32[512]{0:T(512)S(1)}, f32[512]{0:T(512)}, u32[]{:S(2)}) copy-start(f32[512]{0:T(512)} %param.22) | copy-start | bytes 6148
  355.4 19.3 %copy-start.4 = (s32[4096]{0:T(1024)S(1)}, s32[4096]{0:T(1024)}, u32[]{:S(2)}) copy-start(s32[4096]{0:T(1024)} %param.17) | copy-start | bytes 49156
  424.6 10.9 %copy-start.1 = (bf16[512,512]{0,1:T(8,128)(2,1)S(1)}, bf16[512,512]{0,1:T(8,128)(2,1)}, u32[]{:S(2)}) copy-start(bf16[512,512]{0,1:T(8,128)(2,1)} %multiply_convert_fusion) | copy-start | bytes 1572868
  428.9 13.2 %all-to-all-start.2 = ((f32[16,2,1024]{2,1,0:T(2,128)}), f32[16,2,1024]{2,1,0:T(2,128)S(1)}, u32[]{:S(2)}, u32[]{:S(2)}) async-start(f32[16,2,1024]{2,1,0:T(2,128)} %broadcast_in_dim.42), calls=%async_computation.2 | async-start | bytes 262144 | tf_op jit(solution)/shard_map/all_to_all | solution.py:11
Sparse Core Ops, SparseCore 0:
  374.8 41.3 all-gather.1
where the time goes:
time: 451 us; the launch traced here: 450 us
  waiting for transfers between devices  221 us (49%)
  local copies, waits for them, and re-layouts  146 us (32%)
  other arithmetic  23.1 us (5%)
  matrix products  20.3 us (5%)
  between operations  14.3 us (3%)
  blocking collectives  13.9 us (3%)
  starting transfers between devices  11.6 us (3%)
    all_to_all x1, waiting for transfers between devices, per_device(): lax.all_to_all(served, 'neg', split_axis=0, concat_axis=0, tiled=True)  174 us
    gather x1, local copies, waits for them, and re-layouts, per_device(): gathered = message[neighbour_slots]  88.5 us
    gather x1, local copies, waits for them, and re-layouts, per_device(): items_table[lax.all_to_all(fetch_rows, 'neg', split_axis=0, concat_axis=0...  46.5 us
    all_gather x1, waiting for transfers between devices, per_device(): lax.all_gather(negative_embed, 'qry', axis=0, tiled=True)  41.5 us
    reduce_sum x1, other arithmetic, per_device(): jnp.sum(jnp.where(live_mask[:, :, None], gathered, jnp.zeros((), jnp.bflo...  17.6 us
    all_to_all x1, blocking collectives, per_device(): lax.all_to_all(fetch_rows, 'neg', split_axis=0, concat_axis=0, tiled=True)  13.9 us
    dot_general x1, matrix products, make_message(): jnp.dot(rows, message_weight, preferred_element_type=jnp.float32)  10.8 us
  transfers between devices with their start and end apart: 3, of which 3 were waited for; matrix products, arithmetic and copies ran while one was open for 0% of the time, Pallas kernels for 0%

commit v1 on v0

v1 whole, which is shorter than its diff:
```python
import functools
import math

import jax
import jax.numpy as jnp
from jax import lax
from jax.experimental import pallas as pl
from jax.experimental.pallas import tpu as pltpu
from jax.sharding import PartitionSpec as P

LANES = 128
DEAD = 2**31 - 1
CHUNK = 128
STRIDE = 132
BLOCK = 10
STAGE = 1024


def compose_kernel(slots_ref, self_ref, count_ref, fetch_ref, keys_ref):
    neighbours = slots_ref.shape[0]
    columns = slots_ref.shape[1] // LANES
    rows = fetch_ref.shape[0]
    count = count_ref[...]

    def looked_up(slots):
        hi = [s >> 7 for s in slots]
        lo = [s & 127 for s in slots]

        def step(h, found):
            line = jnp.broadcast_to(fetch_ref[pl.ds(h, 1), :], (8, LANES))
            return tuple(
                jnp.where(hi[i] == h, jnp.take_along_axis(line, lo[i], axis=1), found[i])
                for i in range(len(slots))
            )

        found = lax.fori_loop(0, rows, step, tuple(jnp.zeros_like(s) for s in slots))
        return hi, found

    def key_of(hi, row, v):
        part = (hi * 205) >> 10
        return ((part - 8) << 28) | (v << 19) | row

    for j in range(columns):
        lane = slice(j * LANES, (j + 1) * LANES)
        v = lax.broadcasted_iota(jnp.int32, (8, LANES), 1) + j * LANES
        cnt = jnp.broadcast_to(count[:, lane], (8, LANES))
        slots = [slots_ref[8 * i : 8 * (i + 1), lane] for i in range(neighbours // 8)]
        slots.append(jnp.broadcast_to(self_ref[:, lane], (8, LANES)))
        hi, found = looked_up(slots)
        for i in range(neighbours // 8):
            k = lax.broadcasted_iota(jnp.int32, (8, LANES), 0) + 8 * i
            key = key_of(hi[i], found[i], v)
            keys_ref[8 * i : 8 * (i + 1), lane] = jnp.where(k < cnt, key, DEAD)
        own = key_of(hi[-1], found[-1], v) | ((cnt - 20) << 14) | (1 << 13)
        keys_ref[neighbours : neighbours + 1, lane] = own[:1]


def owner_kernel(
    part_ref, list_smem, list_vmem, message_hbm, self_hbm, out_ref,
    table, stage, pick, rows, acc, sems,
):
    entries = 164
    items = message_hbm.shape[0]
    width = message_hbm.shape[1]
    tiles = width // LANES
    per_table = items // STAGE

    def stage_copy(c):
        source = message_hbm if c < per_table else self_hbm
        return pltpu.make_async_copy(
            source.at[pl.ds((c % per_table) * STAGE, STAGE), :], stage.at[c % 2], sems.at[c % 2]
        )

    @pl.when(pl.program_id(0) == 0)
    def _():
        stage_copy(0).start()
        rows[...] = jnp.zeros_like(rows)
        for c in range(2 * per_table):
            if c + 1 < 2 * per_table:
                stage_copy(c + 1).start()
            stage_copy(c).wait()

            def spread(i, _, c=c):
                for u in range(4):
                    at = pl.multiple_of(i * 64 + u * 16, 16)
                    block = stage[c % 2, pl.ds(at, 16), :].astype(jnp.float32)
                    for half in range(2):
                        for j in range(tiles):
                            first = (c * STAGE + at + half * 8) * tiles + j
                            table[pl.ds(first, 8, stride=tiles), :] = block[
                                half * 8 : half * 8 + 8, j * LANES : (j + 1) * LANES
                            ]
                return 0

            lax.fori_loop(0, STAGE // 64, spread, 0)

    part = part_ref[0]
    end = list_smem[0, entries, part]
    start = jnp.where(part == 0, 0, list_smem[0, entries, jnp.maximum(part - 1, 0)])
    row_first = start >> 7
    row_last = (end + 127) >> 7
    negatives = out_ref.shape[0]

    def one_block(base):
        for c in range(BLOCK):
            r = base + c

            @pl.when(r < row_last)
            def _(c=c, r=r):
                line = list_vmem[0, pl.ds(r, 1), :]
                at = r * LANES + lax.broadcasted_iota(jnp.int32, (1, LANES), 1)
                live = (at >= start) & (at < end)
                who = jnp.where(live, (line >> 19) & 511, -1)
                weight = jnp.where((line & 8192) != 0, ((line >> 14) & 31) + 20, 1).astype(jnp.float32)
                v = lax.broadcasted_iota(jnp.int32, (negatives, LANES), 0)
                pick[:, c * LANES : (c + 1) * LANES] = jnp.where(v == who, weight, 0.0).astype(jnp.bfloat16)
                for e in range(CHUNK):
                    t = list_smem[0, r, e] & 16383
                    slab = table[pl.ds(pl.multiple_of(t * tiles, tiles), tiles), :]
                    rows[c, pl.ds(e, tiles, stride=STRIDE), :] = slab

            @pl.when(r >= row_last)
            def _(c=c):
                pick[:, c * LANES : (c + 1) * LANES] = jnp.zeros((negatives, LANES), jnp.bfloat16)

        gathered = jnp.concatenate(
            [
                jnp.concatenate(
                    [rows[c, j * STRIDE : j * STRIDE + CHUNK, :].astype(jnp.bfloat16) for j in range(tiles)],
                    axis=1,
                )
                for c in range(BLOCK)
            ],
            axis=0,
        )
        return jnp.dot(pick[...], gathered, preferred_element_type=jnp.float32)

    acc[...] = one_block(row_first)

    def more(i, _):
        acc[...] += one_block(row_first + i * BLOCK)
        return 0

    lax.fori_loop(1, (row_last - row_first + BLOCK - 1) // BLOCK, more, 0)
    out_ref[...] = acc[...].astype(jnp.bfloat16)


def from_everyone(x, axis):
    devices = lax.axis_size(axis)
    return lax.all_to_all(jnp.broadcast_to(x[None], (devices, *x.shape)), axis, 0, 0, tiled=True)


def composed_keys(neighbour_slots, self_slot, neighbour_count, fetch_rows):
    negatives, neighbours = neighbour_slots.shape
    return pl.pallas_call(
        compose_kernel,
        out_shape=jax.ShapeDtypeStruct((neighbours + 1, negatives), jnp.int32),
        name="compose",
    )(
        neighbour_slots.T,
        self_slot[None, :],
        neighbour_count[None, :],
        fetch_rows.reshape(-1, LANES),
    )


def owner_sums(part, lists, message_part, self_part, negatives):
    devices, lines, _ = lists.shape
    items, width = message_part.shape
    tiles = width // LANES
    return pl.pallas_call(
        owner_kernel,
        grid=(devices,),
        in_specs=[
            pl.BlockSpec(memory_space=pltpu.SMEM),
            pl.BlockSpec((1, lines, LANES), lambda a: (a, 0, 0), memory_space=pltpu.SMEM),
            pl.BlockSpec((1, lines, LANES), lambda a: (a, 0, 0)),
            pl.BlockSpec(memory_space=pl.ANY),
            pl.BlockSpec(memory_space=pl.ANY),
        ],
        out_specs=pl.BlockSpec((negatives, width), lambda a: (a, 0)),
        out_shape=jax.ShapeDtypeStruct((devices * negatives, width), jnp.bfloat16),
        scratch_shapes=[
            pltpu.VMEM((2 * items * tiles, LANES), jnp.float32),
            pltpu.VMEM((2, STAGE, width), jnp.bfloat16),
            pltpu.VMEM((negatives, BLOCK * CHUNK), jnp.bfloat16),
            pltpu.VMEM((BLOCK, tiles * STRIDE, LANES), jnp.float32),
            pltpu.VMEM((negatives, width), jnp.float32),
            pltpu.SemaphoreType.DMA((2,)),
        ],
        compiler_params=pltpu.CompilerParams(
            dimension_semantics=("arbitrary",), vmem_limit_bytes=60 * 2**20
        ),
        name="owner",
    )(part, lists, lists, message_part, self_part)


def per_device(
    items_table,
    fetch_rows,
    neighbour_slots,
    neighbour_count,
    self_slot,
    negative_count,
    message_weight,
    message_bias,
    self_weight,
    neighbour_weight,
    output_bias,
    queries,
):
    f32 = jnp.float32
    negatives = neighbour_count.shape[0]
    parts = lax.axis_size("neg")
    groups = lax.axis_size("qry")
    queries_all = lax.all_gather(queries, "qry", axis=0, tiled=True)

    keys = composed_keys(neighbour_slots, self_slot, neighbour_count, fetch_rows).reshape(-1)
    bounds = jnp.array([min((p + 1 - 8) << 28, DEAD) for p in range(parts)], jnp.int32)
    ends = jnp.sum((keys[None, :] < bounds[:, None]).astype(jnp.int32), axis=1)
    lines = jnp.concatenate([lax.sort(keys, is_stable=False), ends, jnp.zeros((184 * LANES - keys.size - parts,), jnp.int32)])
    lists = from_everyone(lines.reshape(184, LANES), "neg")

    message = jax.nn.relu(
        jnp.dot(items_table, message_weight, preferred_element_type=f32) + message_bias
    ).astype(jnp.bfloat16)
    message_part = jnp.dot(message, neighbour_weight, preferred_element_type=f32).astype(jnp.bfloat16)
    self_part = jnp.dot(items_table, self_weight, preferred_element_type=f32).astype(jnp.bfloat16)

    partial = owner_sums(lax.axis_index("neg").reshape(1).astype(jnp.int32), lists, message_part, self_part, negatives)
    total = lax.psum_scatter(partial, "neg", scatter_dimension=0, tiled=True).astype(f32)

    hidden = jax.nn.relu(total / neighbour_count.astype(f32)[:, None] + output_bias)
    scale_inv = lax.rsqrt(jnp.mean(hidden * hidden, axis=-1, keepdims=True) + 0.25)
    negative_embed = (hidden * scale_inv).astype(jnp.bfloat16)

    own_count = lax.dynamic_slice(negative_count, (lax.axis_index("qry") * negatives,), (negatives,))
    log_count = jnp.log(own_count.astype(f32))
    scores = (
        0.25
        * lax.dot_general(negative_embed, queries_all, (((1,), (1,)), ((), ())), preferred_element_type=f32)
        - log_count[:, None]
    )
    peak = jnp.max(scores, axis=0)
    part_lse = peak + jnp.log(jnp.sum(jnp.exp(scores - peak[None, :]), axis=0))
    shared = jnp.broadcast_to(part_lse.reshape(1, groups, -1), (parts, groups, queries.shape[0]))
    parts_lse = lax.all_to_all(
        shared.reshape(parts * groups, -1), ("neg", "qry"), split_axis=0, concat_axis=0, tiled=True
    )
    top = jnp.max(parts_lse, axis=0)
    query_lse = top + jnp.log(jnp.sum(jnp.exp(parts_lse - top[None, :]), axis=0))
    return (negative_embed, query_lse - math.log(negatives * parts * groups))


def solution(mesh):
    in_specs = (
        P("neg", None),
        P(("neg", "qry"), None),
        P(("neg", "qry"), None),
        P(("neg", "qry")),
        P(("neg", "qry")),
        P("neg"),
        P(),
        P(),
        P(),
        P(),
        P(),
        P("qry", None),
    )
    out_specs = (P(("neg", "qry"), None), P("qry"))
    return jax.shard_map(
        per_device, mesh=mesh, in_specs=in_specs, out_specs=out_specs, check_vma=False
    )
```

time: 451 us -> 284 us (0.63)
  local copies, waits for them, and re-layouts: 146 us -> 5.69 us
  waiting for transfers between devices: 221 us -> 88.3 us
  Pallas kernels: 0 us -> 83.6 us
  matrix products: 20.3 us -> 35.5 us
  blocking collectives: 13.9 us -> 22.4 us
    all_to_all x1 -> x0, waiting for transfers between devices: 174 us -> none  [per_device(): lax.all_to_all(served, 'neg', split_axis=0, concat_axis=0, tiled=True)]
    gather x3 -> x0, local copies, waits for them, and re-layouts: 143 us -> none  [the longest x1 88.5 us: per_device(): gathered = message[neighbour_slots]]
    reduce_scatter x0 -> x1, waiting for transfers between devices: none -> 87.7 us  [per_device(): lax.psum_scatter(partial, 'neg', scatter_dimension=0, tiled=True)]
    pallas_call x0 -> x2, Pallas kernels: none -> 83.6 us  [the longest x1 56.1 us: owner_sums(): pl.pallas_call(owner_kernel, grid=(devices,), in_specs=[pl.BlockSpec(memo...]
    all_gather x1, waiting for transfers between devices: 41.5 us -> 0.03 us  [per_device(): queries_all = lax.all_gather(queries, 'qry', axis=0, tiled=True)]
    dot_general x4 -> x3, matrix products: 20.3 us -> 35.5 us  [the longest x1 13.4 us: per_device(): jnp.dot(message, neighbour_weight, preferred_element_type=f32)]
    reduce_sum x2 -> x4, other arithmetic: 21.2 us -> 12.1 us  [the longest x1 9.55 us: per_device(): part_lse = peak + jnp.log(jnp.sum(jnp.exp(scores - peak[None, :]), axis=0))]
    sort x0 -> x1, other arithmetic: none -> 8.61 us  [per_device(): lax.sort(keys, is_stable=False)]
  transfers between devices with their start and end apart: 3 -> 3, of which waited for: 3 -> 1; matrix products, arithmetic and copies ran while one was open for 0% -> 10% of each run, Pallas kernels for 0% -> 0%
where the time goes in v1:
time: 284 us; the launch traced here: 283 us
  waiting for transfers between devices  88.3 us (31%)
  Pallas kernels  83.6 us (29%)
  matrix products  35.5 us (12%)
  other arithmetic  23.8 us (8%)
  blocking collectives  22.4 us (8%)
  between operations  15.6 us (5%)
  starting transfers between devices  7.84 us (3%)
  local copies, waits for them, and re-layouts  5.69 us (2%)
    reduce_scatter x1, waiting for transfers between devices, per_device(): lax.psum_scatter(partial, 'neg', scatter_dimension=0, tiled=True)  87.7 us
    pallas_call x1, Pallas kernels, owner_sums(): pl.pallas_call(owner_kernel, grid=(devices,), in_specs=[pl.BlockSpec(memo...  56.1 us
    pallas_call x1, Pallas kernels, composed_keys(): pl.pallas_call(compose_kernel, out_shape=jax.ShapeDtypeStruct((neighbours...  27.5 us
    all_to_all x1, blocking collectives, per_device(): lax.all_to_all(shared.reshape(parts * groups, -1), ('neg', 'qry'), split_...  22.4 us
    dot_general x1, matrix products, per_device(): jnp.dot(message, neighbour_weight, preferred_element_type=f32)  13.4 us
    dot_general x1, matrix products, per_device(): lax.dot_general(negative_embed, queries_all, (((1,), (1,)), ((), ())), pr...  12 us
    dot_general x1, matrix products, per_device(): jnp.dot(items_table, self_weight, preferred_element_type=f32)  10.1 us
    reduce_sum x1, other arithmetic, per_device(): part_lse = peak + jnp.log(jnp.sum(jnp.exp(scores - peak[None, :]), axis=0))  9.55 us
  transfers between devices with their start and end apart: 3, of which 1 were waited for; matrix products, arithmetic and copies ran while one was open for 10% of the time, Pallas kernels for 0%

profile of v1, /device:TPU:1, one launch (start us, length us, event | category | flops | bytes accessed | tf_op | source)
XLA Modules:
  0.0 282.7 jit_solution(5557474347436747431)
XLA Ops:
  8.0 0.0 copy-start
  8.0 1.5 reshape.48.fetch_ref
  9.5 27.5 %compose.1 = s32[41,512]{1,0:T(8,128)} custom-call(s32[40,512]{1,0:T(8,128)} %bitcast.19, s32[1,512]{1,0:T(1,128)} %bitcast.21, s32[1,512]{1,0:T(1,128)} %bitcast.20, s32[80,128]{1,0:T(8,128)} %reshape.48.fetch_ref), custom_call_target="tpu_custom_call" | custom-call | tf_op jit(solution)/shard_map/compose/pallas_call | solution.py:155
  37.0 0.9 reshape.49
  37.9 8.6 %sort.7 = s32[20992]{0:T(1024)S(1)} sort(s32[20992]{0:T(1024)S(1)} %reshape.49), dimensions={0}, to_apply=%region_0.0 | sort | flops 314880 | bytes 167936 | tf_op jit(solution)/shard_map/sort | solution.py:221
  46.5 1.0 convert_reduce_fusion
  47.5 0.1 concatenate.3
  47.6 1.3 broadcast_in_dim.16
  48.8 7.6 %all-to-all-start = ((s32[16,184,128]{2,1,0:T(8,128)}), s32[16,184,128]{2,1,0:T(8,128)S(1)}, u32[]{:S(2)}, u32[]{:S(2)}) async-start(s32[16,184,128]{2,1,0:T(8,128)} %broadcast_in_dim.16), calls=%async_computation | async-start | bytes 3014656 | tf_op jit(solution)/shard_map/all_to_all | solution.py:150
  56.4 0.0 copy-start.6
  56.4 0.2 reduce-scatter.2.cloned.1.call-start
  56.7 0.0 copy-done
  56.7 13.4 %convolution_convert_fusion.1.message_hbm = bf16[8192,512]{1,0:T(8,128)(2,1)} fusion(bf16[512,512]{1,0:T(8,128)(2,1)S(1)} %copy-done, bf16[8192,512]{1,0:T(8,128)(2,1)} %param.13, bf16[512,512]{1,0:T(8,128)(2,1)} %param.19, f32[512]{0:T(512)} %param.20), kind=kOutput, calls=%fused_computation.5 | convolution fusion | flops 8606711808 | bytes 17827840 | tf_op jit(solution)/shard_map/dot_general | solution.py:227
  70.0 0.0 copy-done.6
  70.0 10.1 %convolution_convert_fusion.self_hbm = bf16[8192,512]{1,0:T(8,128)(2,1)} fusion(bf16[8192,512]{1,0:T(8,128)(2,1)} %param.13, bf16[512,512]{1,0:T(8,128)(2,1)S(1)} %copy-done.6), kind=kOutput, calls=%fused_computation.4 | convolution fusion | flops 4299161600 | bytes 17301504 | tf_op jit(solution)/shard_map/dot_general | solution.py:228
  80.2 0.0 all-to-all-done.list_smem.list_vmem
  80.2 0.0 copy-start.2
  80.2 1.2 copy-done.2
  81.4 56.1 %owner.1 = bf16[8192,512]{1,0:T(8,128)(2,1)} custom-call(s32[1]{0:T(128)} %bitcast.part_ref, s32[16,184,128]{2,1,0:T(8,128)} %copy-done.2, s32[16,184,128]{2,1,0:T(8,128)} %copy-done.2, bf16[8192,512]{1,0:T(8,128)(2,1)} %convolution_convert_fusion.1.message_hbm, bf16[8192,512]{1,0:T(8,128)(2,1)} %convolution_convert_fusion.self_hbm), custom_call_target="tpu_custom_call" | custom-call | tf_op jit(solution)/shard_map/owner/pallas_call | solution.py:171
  137.5 0.0 copy-start.5
  137.5 0.0 copy-start.4
  137.5 0.0 reduce-scatter.2.cloned.1.call-update
  137.5 0.0 all-gather.2.cloned.1.call-start
  137.6 0.5 all-gather.2.cloned.1.call-update
  138.1 0.1 copy-done.5
  138.1 0.8 convert_log_fusion
  138.9 87.7 %reduce-scatter.2.cloned.1.call-done = bf16[512,512]{1,0:T(8,128)(2,1)} async-done(((bf16[8192,512]{1,0:T(8,128)(2,1)}), bf16[512,512]{1,0:T(8,128)(2,1)}) %reduce-scatter.2.cloned.1.call-update) | async-done | bytes 524304 | tf_op jit(solution)/shard_map/reduce_scatter | solution.py:231
  226.6 0.0 copy-done.4
  226.6 1.4 multiply_reduce_fusion
  228.0 1.3 multiply_convert_fusion
  229.3 0.0 copy-start.3
  229.4 0.0 all-gather.2.cloned.1.call-done
  229.4 12.0 %fusion = (f32[8192]{0:T(1024)S(1)}, f32[512,8192]{1,0:T(8,128)}) fusion(f32[512]{0:T(512)S(1)} %convert_log_fusion, bf16[512,512]{1,0:T(8,128)(2,1)S(1)} %multiply_convert_fusion, bf16[8192,512]{1,0:T(8,128)(2,1)} %all-gather.2.cloned.1.call-done), kind=kOutput, calls=%fused_computation.3 | convolution fusion | flops 4307542016 | bytes 25724928 | tf_op jit(solution)/shard_map/dot_general | solution.py:241
  241.4 0.0 copy-done.3
  241.4 0.0 copy-start.1
  241.4 9.6 %exponential_reduce_fusion = f32[8192]{0:T(1024)S(1)} fusion(f32[512,8192]{1,0:T(8,128)} %get-tuple-element.3, f32[8192]{0:T(1024)S(1)} %get-tuple-element.2, f32[512]{0:T(512)S(1)} %convert_log_fusion), kind=kLoop, calls=%fused_computation | loop fusion | flops 16769024 | bytes 16844800 | tf_op jit(solution)/shard_map/reduce_sum | solution.py:245
  251.1 0.6 all_to_all.12
  251.7 22.4 %all_to_all.17 = f32[128,1,1024]{2,1,0:T(1,128)S(1)} all-to-all(f32[128,1,1024]{2,1,0:T(1,128)S(1)} %all_to_all.12), channel_id=1, replica_groups=mesh['neg'=16,'qry'=8] {'neg','qry'}, dimensions={0} | all-to-all | bytes 1048576 | tf_op jit(solution)/shard_map/all_to_all | solution.py:247
  274.1 0.3 reduce_max.19
  274.5 0.1 fusion.2
  274.6 0.6 add_add_fusion
  275.2 0.0 copy-done.1
  (6 shorter events, 0.1 us)
Async XLA Ops:
  8.0 48.7 %copy-start = (bf16[512,512]{1,0:T(8,128)(2,1)S(1)}, bf16[512,512]{1,0:T(8,128)(2,1)}, u32[]{:S(2)}) copy-start(bf16[512,512]{1,0:T(8,128)(2,1)} %param.22) | copy-start | bytes 1572868
  48.8 31.3 %all-to-all-start = ((s32[16,184,128]{2,1,0:T(8,128)}), s32[16,184,128]{2,1,0:T(8,128)S(1)}, u32[]{:S(2)}, u32[]{:S(2)}) async-start(s32[16,184,128]{2,1,0:T(8,128)} %broadcast_in_dim.16), calls=%async_computation | async-start | bytes 3014656 | tf_op jit(solution)/shard_map/all_to_all | solution.py:150
  56.4 13.6 %copy-start.6 = (bf16[512,512]{1,0:T(8,128)(2,1)S(1)}, bf16[512,512]{1,0:T(8,128)(2,1)}, u32[]{:S(2)}) copy-start(bf16[512,512]{1,0:T(8,128)(2,1)} %param.21) | copy-start | bytes 1572868
  56.4 170.2 %reduce-scatter.2.cloned.1.call-start = ((), (), s32[]{:S(2)}) async-start(), calls=%async_computation.3 | async-start | bytes 8912896 | tf_op jit(solution)/shard_map/reduce_scatter | solution.py:231
  80.2 1.2 copy-start.2
  137.5 0.7 copy-start.5
  137.5 89.1 %copy-start.4 = (f32[512]{0:T(512)S(1)}, f32[512]{0:T(512)}, u32[]{:S(2)}) copy-start(f32[512]{0:T(512)} %param.23) | copy-start | bytes 6148
  137.5 91.9 %all-gather.2.cloned.1.call-start = ((), (), s32[]{:S(2)}) async-start(), calls=%async_computation.4 | async-start | bytes 9437184 | tf_op jit(solution)/shard_map/all_gather | solution.py:216
  229.3 12.1 %copy-start.3 = (bf16[512,512]{1,0:T(8,128)(2,1)}, bf16[512,512]{1,0:T(8,128)(2,1)S(1)}, u32[]{:S(2)}) copy-start(bf16[512,512]{1,0:T(8,128)(2,1)S(1)} %multiply_convert_fusion) | copy-start | bytes 1572868
  241.4 33.8 %copy-start.1 = (bf16[512,512]{1,0:T(8,128)(2,1)S(1)}, bf16[512,512]{1,0:T(8,128)(2,1)}, u32[]{:S(2)}) copy-start(bf16[512,512]{1,0:T(8,128)(2,1)} %param.22) | copy-start | bytes 1572868
Sparse Core Ops, SparseCore 0:
  137.6 88.9 reduce-scatter.1
Sparse Core Ops, SparseCore 1:
  139.7 54.7 all-gather.1

commit v2 on v1

--- a/solution.py
+++ b/solution.py
@@ -16,54 +16,68 @@
 STAGE = 1024
 
 
-def compose_kernel(slots_ref, self_ref, count_ref, fetch_ref, keys_ref):
-    neighbours = slots_ref.shape[0]
-    columns = slots_ref.shape[1] // LANES
-    rows = fetch_ref.shape[0]
-    count = count_ref[...]
-
-    def looked_up(slots):
-        hi = [s >> 7 for s in slots]
-        lo = [s & 127 for s in slots]
-
-        def step(h, found):
-            line = jnp.broadcast_to(fetch_ref[pl.ds(h, 1), :], (8, LANES))
-            return tuple(
-                jnp.where(hi[i] == h, jnp.take_along_axis(line, lo[i], axis=1), found[i])
-                for i in range(len(slots))
-            )
-
-        found = lax.fori_loop(0, rows, step, tuple(jnp.zeros_like(s) for s in slots))
-        return hi, found
-
-    def key_of(hi, row, v):
-        part = (hi * 205) >> 10
-        return ((part - 8) << 28) | (v << 19) | row
-
-    for j in range(columns):
-        lane = slice(j * LANES, (j + 1) * LANES)
-        v = lax.broadcasted_iota(jnp.int32, (8, LANES), 1) + j * LANES
-        cnt = jnp.broadcast_to(count[:, lane], (8, LANES))
-        slots = [slots_ref[8 * i : 8 * (i + 1), lane] for i in range(neighbours // 8)]
-        slots.append(jnp.broadcast_to(self_ref[:, lane], (8, LANES)))
-        hi, found = looked_up(slots)
+def compose_kernel(slots_ref, self_ref, count_ref, own_count_ref, fetch_ref, keys_ref):
+    neighbours, negatives = slots_ref.shape
+    parts, per_part = fetch_ref.shape
+    per_line = per_part // LANES
+    half = parts // 2
+    packed = fetch_ref[:half, :] | (fetch_ref[half:, :] << 13)
+    lines = [
+        jnp.broadcast_to(packed[p : p + 1, j * LANES : (j + 1) * LANES], (8, LANES))
+        for p in range(half)
+        for j in range(per_line)
+    ]
+
+    def located(slot):
+        hi = slot >> 7
+        lo = slot & 127
+        upper = hi >= len(lines)
+        folded = jnp.where(upper, hi - len(lines), hi)
+        found = jnp.zeros_like(slot)
+        for h, line in enumerate(lines):
+            at = jnp.take_along_axis(line, lo, axis=1, mode="promise_in_bounds")
+            found = jnp.where(folded == h, at, found)
+        row = jnp.where(upper, found >> 13, found & 8191)
+        return ((((hi * 205) >> 10) - 8) << 28) | row
+
+    sublane = lax.broadcasted_iota(jnp.int32, (8, LANES), 0)
+    lane = lax.broadcasted_iota(jnp.int32, (8, LANES), 1)
+    for j in range(negatives // LANES):
+        cols = slice(j * LANES, (j + 1) * LANES)
+        count = jnp.broadcast_to(count_ref[:, cols], (8, LANES))
         for i in range(neighbours // 8):
-            k = lax.broadcasted_iota(jnp.int32, (8, LANES), 0) + 8 * i
-            key = key_of(hi[i], found[i], v)
-            keys_ref[8 * i : 8 * (i + 1), lane] = jnp.where(k < cnt, key, DEAD)
-        own = key_of(hi[-1], found[-1], v) | ((cnt - 20) << 14) | (1 << 13)
-        keys_ref[neighbours : neighbours + 1, lane] = own[:1]
+            key = located(slots_ref[8 * i : 8 * (i + 1), cols]) | ((lane + j * LANES) << 19)
+            first = (j * (neighbours // 8) + i) * 8
+            keys_ref[first : first + 8, :] = jnp.where(sublane + 8 * i < count, key, DEAD)
+    own = located(self_ref[...]) | ((sublane * LANES + lane) << 19)
+    own = own | ((own_count_ref[...] - 20) << 14) | (1 << 13)
+    keys_ref[neighbours * negatives // LANES :, :] = own[: negatives // LANES]
 
 
 def owner_kernel(
-    part_ref, list_smem, list_vmem, message_hbm, self_hbm, out_ref,
-    table, stage, pick, rows, acc, sems,
+    part_ref, ends_ref, lists_ref, message_hbm, self_hbm, out_ref,
+    table, stage, pick, rows, acc, offsets, places, sems, place_sems,
 ):
-    entries = 164
     items = message_hbm.shape[0]
     width = message_hbm.shape[1]
     tiles = width // LANES
     per_table = items // STAGE
+    a = pl.program_id(0)
+    devices = pl.num_programs(0)
+    part = part_ref[0]
+    negatives = out_ref.shape[0]
+
+    def range_of(r):
+        return jnp.where(part == 0, 0, ends_ref[r, jnp.maximum(part - 1, 0)]), ends_ref[r, part]
+
+    def place_copy(slot):
+        return pltpu.make_async_copy(offsets.at[slot], places.at[slot], place_sems.at[slot])
+
+    def place(r, base, slot):
+        for c in range(BLOCK):
+            line = lists_ref[r, pl.ds(base + c, 1), :]
+            offsets[slot, c : c + 1, :] = (line & 16383) * tiles
+        place_copy(slot).start()
 
     def stage_copy(c):
         source = message_hbm if c < per_table else self_hbm
@@ -71,9 +85,10 @@
             source.at[pl.ds((c % per_table) * STAGE, STAGE), :], stage.at[c % 2], sems.at[c % 2]
         )
 
-    @pl.when(pl.program_id(0) == 0)
+    @pl.when(a == 0)
     def _():
         stage_copy(0).start()
+        place(0, range_of(0)[0] >> 7, 0)
         rows[...] = jnp.zeros_like(rows)
         for c in range(2 * per_table):
             if c + 1 < 2 * per_table:
@@ -94,30 +109,27 @@
 
             lax.fori_loop(0, STAGE // 64, spread, 0)
 
-    part = part_ref[0]
-    end = list_smem[0, entries, part]
-    start = jnp.where(part == 0, 0, list_smem[0, entries, jnp.maximum(part - 1, 0)])
+    start, end = range_of(a)
     row_first = start >> 7
     row_last = (end + 127) >> 7
-    negatives = out_ref.shape[0]
-
-    def one_block(base):
+
+    def one_block(base, slot):
+        place_copy(slot).wait()
+        v = lax.broadcasted_iota(jnp.int32, (negatives, LANES), 0)
+        lane = lax.broadcasted_iota(jnp.int32, (1, LANES), 1)
         for c in range(BLOCK):
             r = base + c
 
             @pl.when(r < row_last)
             def _(c=c, r=r):
-                line = list_vmem[0, pl.ds(r, 1), :]
-                at = r * LANES + lax.broadcasted_iota(jnp.int32, (1, LANES), 1)
-                live = (at >= start) & (at < end)
-                who = jnp.where(live, (line >> 19) & 511, -1)
+                line = lists_ref[a, pl.ds(r, 1), :]
+                at = r * LANES + lane
+                who = jnp.where((at >= start) & (at < end), (line >> 19) & 511, -1)
                 weight = jnp.where((line & 8192) != 0, ((line >> 14) & 31) + 20, 1).astype(jnp.float32)
-                v = lax.broadcasted_iota(jnp.int32, (negatives, LANES), 0)
                 pick[:, c * LANES : (c + 1) * LANES] = jnp.where(v == who, weight, 0.0).astype(jnp.bfloat16)
                 for e in range(CHUNK):
-                    t = list_smem[0, r, e] & 16383
-                    slab = table[pl.ds(pl.multiple_of(t * tiles, tiles), tiles), :]
-                    rows[c, pl.ds(e, tiles, stride=STRIDE), :] = slab
+                    at = pl.multiple_of(places[slot, c, e], tiles)
+                    rows[c, pl.ds(e, tiles, stride=STRIDE), :] = table[pl.ds(at, tiles), :]
 
             @pl.when(r >= row_last)
             def _(c=c):
@@ -135,10 +147,17 @@
         )
         return jnp.dot(pick[...], gathered, preferred_element_type=jnp.float32)
 
-    acc[...] = one_block(row_first)
+    slot = a % 2
+
+    @pl.when(a + 1 < devices)
+    def _():
+        place(a + 1, range_of(a + 1)[0] >> 7, 1 - slot)
+
+    acc[...] = one_block(row_first, slot)
 
     def more(i, _):
-        acc[...] += one_block(row_first + i * BLOCK)
+        place(a, row_first + i * BLOCK, slot)
+        acc[...] += one_block(row_first + i * BLOCK, slot)
         return 0
 
     lax.fori_loop(1, (row_last - row_first + BLOCK - 1) // BLOCK, more, 0)
@@ -152,19 +171,25 @@
 
 def composed_keys(neighbour_slots, self_slot, neighbour_count, fetch_rows):
     negatives, neighbours = neighbour_slots.shape
+    folded = negatives // LANES
+
+    def tile_of(x):
+        return jnp.pad(x.reshape(folded, LANES), ((0, 8 - folded), (0, 0)))
+
     return pl.pallas_call(
         compose_kernel,
-        out_shape=jax.ShapeDtypeStruct((neighbours + 1, negatives), jnp.int32),
+        out_shape=jax.ShapeDtypeStruct(((neighbours + 1) * folded, LANES), jnp.int32),
         name="compose",
     )(
         neighbour_slots.T,
-        self_slot[None, :],
+        tile_of(self_slot),
         neighbour_count[None, :],
-        fetch_rows.reshape(-1, LANES),
-    )
-
-
-def owner_sums(part, lists, message_part, self_part, negatives):
+        tile_of(neighbour_count),
+        fetch_rows,
+    )
+
+
+def owner_sums(part, ends, lists, message_part, self_part, negatives):
     devices, lines, _ = lists.shape
     items, width = message_part.shape
     tiles = width // LANES
@@ -173,8 +198,8 @@
         grid=(devices,),
         in_specs=[
             pl.BlockSpec(memory_space=pltpu.SMEM),
-            pl.BlockSpec((1, lines, LANES), lambda a: (a, 0, 0), memory_space=pltpu.SMEM),
-            pl.BlockSpec((1, lines, LANES), lambda a: (a, 0, 0)),
+            pl.BlockSpec(memory_space=pltpu.SMEM),
+            pl.BlockSpec(memory_space=pltpu.VMEM),
             pl.BlockSpec(memory_space=pl.ANY),
             pl.BlockSpec(memory_space=pl.ANY),
         ],
@@ -186,13 +211,16 @@
             pltpu.VMEM((negatives, BLOCK * CHUNK), jnp.bfloat16),
             pltpu.VMEM((BLOCK, tiles * STRIDE, LANES), jnp.float32),
             pltpu.VMEM((negatives, width), jnp.float32),
+            pltpu.VMEM((2, 16, LANES), jnp.int32),
+            pltpu.SMEM((2, 16, LANES), jnp.int32),
+            pltpu.SemaphoreType.DMA((2,)),
             pltpu.SemaphoreType.DMA((2,)),
         ],
         compiler_params=pltpu.CompilerParams(
             dimension_semantics=("arbitrary",), vmem_limit_bytes=60 * 2**20
         ),
         name="owner",
-    )(part, lists, lists, message_part, self_part)
+    )(part, ends, lists, message_part, self_part)
 
 
 def per_device(
@@ -227,7 +255,8 @@
     message_part = jnp.dot(message, neighbour_weight, preferred_element_type=f32).astype(jnp.bfloat16)
     self_part = jnp.dot(items_table, self_weight, preferred_element_type=f32).astype(jnp.bfloat16)
 
-    partial = owner_sums(lax.axis_index("neg").reshape(1).astype(jnp.int32), lists, message_part, self_part, negatives)
+    part = lax.axis_index("neg").reshape(1).astype(jnp.int32)
+    partial = owner_sums(part, lists[:, keys.size // LANES, :parts], lists, message_part, self_part, negatives)
     total = lax.psum_scatter(partial, "neg", scatter_dimension=0, tiled=True).astype(f32)
 
     hidden = jax.nn.relu(total / neighbour_count.astype(f32)[:, None] + output_bias)

time: 284 us -> 252 us (0.89)
  Pallas kernels: 83.6 us -> 51.4 us
    pallas_call x1, Pallas kernels: 27.5 us -> 2.57 us  [composed_keys(): pl.pallas_call(compose_kernel, out_shape=jax.ShapeDtypeStruct(((neighbour...]
    pallas_call x1, Pallas kernels: 56.1 us -> 48.8 us  [owner_sums(): pl.pallas_call(owner_kernel, grid=(devices,), in_specs=[pl.BlockSpec(memo...]
  transfers between devices with their start and end apart: 3 -> 3, of which waited for: 1 -> 1; matrix products, arithmetic and copies ran while one was open for 10% -> 11% of each run, Pallas kernels for 0% -> 0%
where the time goes in v2:
time: 252 us; the launch traced here: 251 us
  waiting for transfers between devices  87.6 us (35%)
  Pallas kernels  51.4 us (20%)
  matrix products  35.4 us (14%)
  other arithmetic  24.6 us (10%)
  blocking collectives  22.5 us (9%)
  between operations  15.6 us (6%)
  starting transfers between devices  8.06 us (3%)
  local copies, waits for them, and re-layouts  5.95 us (2%)
    reduce_scatter x1, waiting for transfers between devices, per_device(): lax.psum_scatter(partial, 'neg', scatter_dimension=0, tiled=True)  87.2 us
    pallas_call x1, Pallas kernels, owner_sums(): pl.pallas_call(owner_kernel, grid=(devices,), in_specs=[pl.BlockSpec(memo...  48.8 us
    all_to_all x1, blocking collectives, per_device(): lax.all_to_all(shared.reshape(parts * groups, -1), ('neg', 'qry'), split_...  22.5 us
    dot_general x1, matrix products, per_device(): jnp.dot(message, neighbour_weight, preferred_element_type=f32)  13.4 us
    dot_general x1, matrix products, per_device(): lax.dot_general(negative_embed, queries_all, (((1,), (1,)), ((), ())), pr...  11.9 us
    dot_general x1, matrix products, per_device(): jnp.dot(items_table, self_weight, preferred_element_type=f32)  10.1 us
    reduce_sum x1, other arithmetic, per_device(): part_lse = peak + jnp.log(jnp.sum(jnp.exp(scores - peak[None, :]), axis=0))  9.55 us
    sort x1, other arithmetic, per_device(): lax.sort(keys, is_stable=False)  9.26 us
  transfers between devices with their start and end apart: 3, of which 1 were waited for; matrix products, arithmetic and copies ran while one was open for 11% of the time, Pallas kernels for 0%

profile of v2, /device:TPU:1, one launch (start us, length us, event | category | flops | bytes accessed | tf_op | source)
XLA Modules:
  0.0 251.1 jit_solution(2396696139493627390)
XLA Ops:
  8.0 0.0 copy-start
  8.0 1.3 pad.7.self_ref
  9.3 1.3 pad.8.own_count_ref
  10.6 2.6 %compose.1 = s32[164,128]{1,0:T(8,128)} custom-call(s32[40,512]{1,0:T(8,128)} %bitcast.24, s32[8,128]{1,0:T(8,128)} %pad.7.self_ref, s32[1,512]{1,0:T(1,128)} %bitcast.27, s32[8,128]{1,0:T(8,128)} %pad.8.own_count_ref, s32[16,640]{1,0:T(8,128)} %fetch_ref.1), custom_call_target="tpu_custom_call" | custom-call | tf_op jit(solution)/shard_map/compose/pallas_call | solution.py:179
  13.2 9.3 %sort.7 = s32[20992]{0:T(1024)S(1)} sort(s32[20992]{0:T(1024)} %bitcast.21), dimensions={0}, to_apply=%region_0.1 | sort | flops 314880 | bytes 167936 | tf_op jit(solution)/shard_map/sort | solution.py:249
  22.5 1.2 convert_reduce_fusion
  23.7 0.1 concatenate.3
  23.8 1.3 broadcast_in_dim.13
  25.0 7.6 %all-to-all-start = ((s32[16,184,128]{2,1,0:T(8,128)}), s32[16,184,128]{2,1,0:T(8,128)S(1)}, u32[]{:S(2)}, u32[]{:S(2)}) async-start(s32[16,184,128]{2,1,0:T(8,128)} %broadcast_in_dim.13), calls=%async_computation | async-start | bytes 3014656 | tf_op jit(solution)/shard_map/all_to_all | solution.py:169
  32.6 0.0 copy-start.6
  32.6 0.2 reduce-scatter.2.cloned.1.call-start
  32.9 0.0 copy-done
  32.9 13.4 %convolution_convert_fusion.1.message_hbm = bf16[8192,512]{1,0:T(8,128)(2,1)} fusion(bf16[512,512]{1,0:T(8,128)(2,1)S(1)} %copy-done, bf16[8192,512]{1,0:T(8,128)(2,1)} %param.13, bf16[512,512]{1,0:T(8,128)(2,1)} %param.19, f32[512]{0:T(512)} %param.20), kind=kOutput, calls=%fused_computation.5 | convolution fusion | flops 8606711808 | bytes 17827840 | tf_op jit(solution)/shard_map/dot_general | solution.py:255
  46.2 0.0 copy-done.6
  46.2 10.1 %convolution_convert_fusion.self_hbm = bf16[8192,512]{1,0:T(8,128)(2,1)} fusion(bf16[8192,512]{1,0:T(8,128)(2,1)} %param.13, bf16[512,512]{1,0:T(8,128)(2,1)S(1)} %copy-done.6), kind=kOutput, calls=%fused_computation.4 | convolution fusion | flops 4299161600 | bytes 17301504 | tf_op jit(solution)/shard_map/dot_general | solution.py:256
  56.4 0.0 all-to-all-done.lists_ref
  56.4 0.0 copy-start.2
  56.4 0.7 slice.4
  57.0 0.6 copy-done.2
  57.6 48.8 %owner.1 = bf16[8192,512]{1,0:T(8,128)(2,1)} custom-call(s32[1]{0:T(128)} %bitcast.part_ref, s32[16,16]{1,0:T(8,128)} %bitcast.25, s32[16,184,128]{2,1,0:T(8,128)} %copy-done.2, bf16[8192,512]{1,0:T(8,128)(2,1)} %convolution_convert_fusion.1.message_hbm, bf16[8192,512]{1,0:T(8,128)(2,1)} %convolution_convert_fusion.self_hbm), custom_call_target="tpu_custom_call" | custom-call | tf_op jit(solution)/shard_map/owner/pallas_call | solution.py:196
  106.4 0.0 copy-start.4
  106.5 0.0 copy-start.5
  106.5 0.0 reduce-scatter.2.cloned.1.call-update
  106.5 0.3 all-gather.2.cloned.1.call-start
  106.8 0.3 all-gather.2.cloned.1.call-update
  107.1 0.1 copy-done.4
  107.1 0.8 convert_log_fusion
  107.9 87.2 %reduce-scatter.2.cloned.1.call-done = bf16[512,512]{1,0:T(8,128)(2,1)} async-done(((bf16[8192,512]{1,0:T(8,128)(2,1)}), bf16[512,512]{1,0:T(8,128)(2,1)}) %reduce-scatter.2.cloned.1.call-update) | async-done | bytes 524304 | tf_op jit(solution)/shard_map/reduce_scatter | solution.py:260
  195.1 0.0 copy-done.5
  195.1 1.4 multiply_reduce_fusion
  196.5 1.3 multiply_convert_fusion
  197.9 0.0 copy-start.3
  197.9 0.0 all-gather.2.cloned.1.call-done
  197.9 11.9 %fusion = (f32[8192]{0:T(1024)S(1)}, f32[512,8192]{1,0:T(8,128)}) fusion(f32[512]{0:T(512)S(1)} %convert_log_fusion, bf16[512,512]{1,0:T(8,128)(2,1)S(1)} %multiply_convert_fusion, bf16[8192,512]{1,0:T(8,128)(2,1)} %all-gather.2.cloned.1.call-done), kind=kOutput, calls=%fused_computation.3 | convolution fusion | flops 4307542016 | bytes 25724928 | tf_op jit(solution)/shard_map/dot_general | solution.py:270
  209.8 0.0 copy-done.3
  209.8 0.0 copy-start.1
  209.8 9.6 %exponential_reduce_fusion = f32[8192]{0:T(1024)S(1)} fusion(f32[512,8192]{1,0:T(8,128)} %get-tuple-element.3, f32[8192]{0:T(1024)S(1)} %get-tuple-element.2, f32[512]{0:T(512)S(1)} %convert_log_fusion), kind=kLoop, calls=%fused_computation | loop fusion | flops 16769024 | bytes 16844800 | tf_op jit(solution)/shard_map/reduce_sum | solution.py:274
  219.5 0.6 all_to_all.12
  220.1 22.5 %all_to_all.17 = f32[128,1,1024]{2,1,0:T(1,128)S(1)} all-to-all(f32[128,1,1024]{2,1,0:T(1,128)S(1)} %all_to_all.12), channel_id=1, replica_groups=mesh['neg'=16,'qry'=8] {'neg','qry'}, dimensions={0} | all-to-all | bytes 1048576 | tf_op jit(solution)/shard_map/all_to_all | solution.py:276
  242.6 0.3 reduce_max.19
  242.9 0.1 fusion.2
  243.1 0.6 add_add_fusion
  243.7 0.0 copy-done.1
  (6 shorter events, 0.1 us)
Async XLA Ops:
  8.0 24.9 %copy-start = (bf16[512,512]{1,0:T(8,128)(2,1)S(1)}, bf16[512,512]{1,0:T(8,128)(2,1)}, u32[]{:S(2)}) copy-start(bf16[512,512]{1,0:T(8,128)(2,1)} %param.22) | copy-start | bytes 1572868
  25.0 31.3 %all-to-all-start = ((s32[16,184,128]{2,1,0:T(8,128)}), s32[16,184,128]{2,1,0:T(8,128)S(1)}, u32[]{:S(2)}, u32[]{:S(2)}) async-start(s32[16,184,128]{2,1,0:T(8,128)} %broadcast_in_dim.13), calls=%async_computation | async-start | bytes 3014656 | tf_op jit(solution)/shard_map/all_to_all | solution.py:169
  32.6 13.6 %copy-start.6 = (bf16[512,512]{1,0:T(8,128)(2,1)S(1)}, bf16[512,512]{1,0:T(8,128)(2,1)}, u32[]{:S(2)}) copy-start(bf16[512,512]{1,0:T(8,128)(2,1)} %param.21) | copy-start | bytes 1572868
  32.6 162.5 %reduce-scatter.2.cloned.1.call-start = ((), (), s32[]{:S(2)}) async-start(), calls=%async_computation.3 | async-start | bytes 8912896 | tf_op jit(solution)/shard_map/reduce_scatter | solution.py:260
  56.4 1.2 copy-start.2
  106.4 0.7 copy-start.4
  106.5 88.7 %copy-start.5 = (f32[512]{0:T(512)S(1)}, f32[512]{0:T(512)}, u32[]{:S(2)}) copy-start(f32[512]{0:T(512)} %param.23) | copy-start | bytes 6148
  106.5 91.4 %all-gather.2.cloned.1.call-start = ((), (), s32[]{:S(2)}) async-start(), calls=%async_computation.4 | async-start | bytes 9437184 | tf_op jit(solution)/shard_map/all_gather | solution.py:244
  197.9 11.9 %copy-start.3 = (bf16[512,512]{1,0:T(8,128)(2,1)}, bf16[512,512]{1,0:T(8,128)(2,1)S(1)}, u32[]{:S(2)}) copy-start(bf16[512,512]{1,0:T(8,128)(2,1)S(1)} %multiply_convert_fusion) | copy-start | bytes 1572868
  209.8 33.9 %copy-start.1 = (bf16[512,512]{1,0:T(8,128)(2,1)S(1)}, bf16[512,512]{1,0:T(8,128)(2,1)}, u32[]{:S(2)}) copy-start(bf16[512,512]{1,0:T(8,128)(2,1)} %param.22) | copy-start | bytes 1572868
Sparse Core Ops, SparseCore 0:
  106.6 88.4 reduce-scatter.1
Sparse Core Ops, SparseCore 1:
  108.7 54.2 all-gather.1
